TPU v7x, 32 devices: a whole 2x2x4 slice. The times are simulated.
32 devices in a mesh: dp: 4 (over z), vocab: 8 (over y, x, core).
Axes of the slice: x: 2, y: 2, z: 4, core: 2. Of those that a mesh axis runs over, the one named last changes fastest.
Arguments:
- hidden: bfloat16 [32, 14, 4096], P('dp', None, 'vocab'), may hold values from -400 to 400
- weight: bfloat16 [4096, 16032], P(None, ('dp', 'vocab')), may hold values from -0.09375 to 0.09375
- targets: int32 [32, 14], P('dp'), may hold values from 0 to 16031
- lengths: int32 [4, 8], P('dp'), may hold values from 1 to 14, 56 in all within a row
- rewards: int32 [4, 8], P('dp'), may hold values from -256 to 256
- arrival: int32 [32], replicated, may hold values from 0 to 31, each once
Outputs:
- token_logprobs: float32 [32, 14], P('dp')
- advantages: float32 [32], P('dp')
- weighted: float32 [32], P('dp')
Inputs may be any that keep to these rules, and one draw needn't show every extreme that they name: The lengths of one device's 8 completions sum to exactly 56, and one of them is 14. `arrival`: every completion number appears once; completion p * 8 + j is sample j of prompt p.
All inputs are finite; a program needn't handle non-finite values.
Results may differ from a plain program's by a relative error of at most 0.0003.
Values may be sent and summed in bfloat16 or wider, within the bound.
A program may use at most 192 MiB of HBM per device.

v0:
```python
import jax
import jax.numpy as jnp
from jax import lax
from jax.sharding import PartitionSpec as P

SAMPLES = 8
reward_unit = 1.0 / 64.0


def combined_all(value, axis, join):
    pieces = jax.tree.map(lambda part: lax.all_gather(part, axis), value)
    head = jax.tree.map(lambda part: part[0], pieces)
    tail = jax.tree.map(lambda part: part[1:], pieces)
    subtotal, _ = lax.scan(lambda subtotal, share: (join(subtotal, share), None), head, tail)
    return subtotal


def merge_totals(first, second):
    highest = jnp.maximum(first[0], second[0])
    totals = first[1] * jnp.exp(first[0] - highest) + second[1] * jnp.exp(second[0] - highest)
    return (highest, totals, first[2] + second[2])


def local(hidden, weight, targets, lengths, rewards, arrival):
    dp_count = lax.axis_size("dp")
    vocab_count = lax.axis_size("vocab")
    per_device = hidden.shape[0]
    window = hidden.shape[1]
    shard_width = weight.shape[1]
    completions = per_device * dp_count
    owner = lax.axis_index("dp")
    first_column = (owner * vocab_count + lax.axis_index("vocab")) * shard_width
    all_lengths, all_rewards = (
        lax.all_gather(lengths, "dp", axis=0, tiled=True),
        lax.all_gather(rewards, "dp", axis=0, tiled=True),
    )
    features = lax.all_gather(hidden, "vocab", axis=2, tiled=True)
    model_width = features.shape[2]
    column_ids = lax.iota(jnp.int32, shard_width)
    position_ids = lax.iota(jnp.int32, window)
    slot_ids = lax.iota(jnp.int32, completions)
    matching = arrival[None, :] == slot_ids[:, None]

    def lookup(table):
        return jnp.sum(jnp.where(matching, table[None, :], 0), axis=1)

    slot_of = lookup(slot_ids)
    length_of = lookup(all_lengths.reshape(completions))
    reward_of = lookup(all_rewards.reshape(completions)).astype(jnp.float32) * reward_unit
    shard_part = (
        lax.all_gather(features, "dp", axis=0, tiled=True),
        lax.all_gather(targets, "dp", axis=0, tiled=True),
    )
    count = shard_part[0].shape[0] * window
    row_block = shard_part[0].reshape(count, model_width)
    logits = jnp.dot(row_block, weight, preferred_element_type=jnp.float32)
    highest = jnp.max(logits, axis=1)
    totals = jnp.sum(jnp.exp(logits - highest[:, None]), axis=1)
    local_ids = shard_part[1].reshape(count) - first_column
    picked = jnp.sum(jnp.where(column_ids[None, :] == local_ids[:, None], logits, 0.0), axis=1)
    stats = (highest, totals, picked)
    stats = (stats[0], stats[1], stats[2])
    base_of = slot_of * window
    usable = position_ids[None, :] < length_of[:, None]
    source_rows = jnp.where(usable, base_of[:, None] + position_ids[None, :], 0)
    my_usable = lax.dynamic_slice_in_dim(usable, owner * per_device, per_device, 0)
    ordered_high = stats[0][source_rows].reshape(dp_count, per_device * window)
    ordered_totals = stats[1][source_rows].reshape(dp_count, per_device * window)
    ordered_picked = stats[2][source_rows].reshape(dp_count, per_device * window)
    arrived = (
        lax.all_to_all(ordered_high, "dp", split_axis=0, concat_axis=0, tiled=True),
        lax.all_to_all(ordered_totals, "dp", split_axis=0, concat_axis=0, tiled=True),
        lax.all_to_all(ordered_picked, "dp", split_axis=0, concat_axis=0, tiled=True),
    )
    highest = jnp.max(arrived[0], axis=0)
    totals = jnp.sum(arrived[1] * jnp.exp(arrived[0] - highest[None, :]), axis=0)
    picked = jnp.sum(arrived[2], axis=0)
    highest, totals, picked = combined_all((highest, totals, picked), "vocab", merge_totals)
    highest = highest.reshape(per_device, window)
    totals = totals.reshape(per_device, window)
    picked = picked.reshape(per_device, window)
    token_logprobs = jnp.where(my_usable, picked - highest - jnp.log(totals), 0.0)
    my_rewards = lax.dynamic_slice_in_dim(reward_of, owner * per_device, per_device, 0)
    my_lengths = lax.dynamic_slice_in_dim(length_of, owner * per_device, per_device, 0)
    groups = jnp.sum(my_rewards.reshape(per_device // SAMPLES, SAMPLES), axis=1)
    advantages = my_rewards - (jnp.repeat(groups, SAMPLES) - my_rewards) / (SAMPLES - 1.0)
    weighted = advantages * jnp.sum(token_logprobs, axis=1) / my_lengths.astype(jnp.float32)
    return (token_logprobs, advantages, weighted)


def solution(mesh):
    return jax.shard_map(
        local,
        mesh=mesh,
        in_specs=(
            P("dp", None, "vocab"),
            P(None, ("dp", "vocab")),
            P("dp", None),
            P("dp", None),
            P("dp", None),
            P(),
        ),
        out_specs=(P("dp", None), P("dp"), P("dp")),
        check_vma=False,
    )
```

profile of v0, /device:TPU:0, one launch (start us, length us, event | category | flops | bytes accessed | tf_op | source)
XLA Modules:
  0.0 175.6 jit_solution(2976874843851512155)
XLA Ops:
  7.2 0.0 all-gather.7.cloned.1.call-start
  7.2 14.2 %all_gather.34 = bf16[8,14,4096]{2,0,1:T(8,128)(2,1)} all-gather(bf16[8,14,512]{2,0,1:T(8,128)(2,1)} %param.8), channel_id=1, replica_groups=mesh['dp'=4,'vocab'=8] {'vocab'}, dimensions={2}, use_global_device_ids=true | all-gather | bytes 1032192 | tf_op jit(solution)/shard_map/all_gather | solution.py:37
  21.4 0.0 all-gather.7.cloned.1.call-update
  21.4 11.3 %all-gather.4 = s32[4,1,8]{2,1,0:T(1,128)S(1)} all-gather(s32[1,1,8]{2,1,0:T(1,128)} %bitcast.32), channel_id=1, replica_groups=mesh['dp'=4,'vocab'=8] {'dp'}, dimensions={0}, use_global_device_ids=true | all-gather | bytes 160 | tf_op jit(solution)/shard_map/all_gather | solution.py:35
  32.7 8.2 %all-gather.3 = s32[4,1,8]{2,1,0:T(1,128)S(1)} all-gather(s32[1,1,8]{2,1,0:T(1,128)} %bitcast.33), channel_id=1, replica_groups=mesh['dp'=4,'vocab'=8] {'dp'}, dimensions={0}, use_global_device_ids=true | all-gather | bytes 160 | tf_op jit(solution)/shard_map/all_gather | solution.py:34
  40.9 0.5 broadcast.116
  41.4 0.7 reduce.11
  42.1 0.1 broadcast_in_dim.62
  42.2 0.7 reduce.10
  42.9 0.1 broadcast_in_dim.55
  42.9 0.8 select_reduce_fusion.1
  43.8 0.1 compare_select_fusion
  43.8 0.1 reshape.126
  43.9 14.1 %all_gather.40 = s32[32,14]{1,0:T(8,128)S(1)} all-gather(s32[8,14]{1,0:T(8,128)} %param.10), channel_id=1, replica_groups=mesh['dp'=4,'vocab'=8] {'dp'}, dimensions={0}, use_global_device_ids=true | all-gather | bytes 2240 | tf_op jit(solution)/shard_map/all_gather | solution.py:52
  58.0 0.1 sub.57
  58.1 36.0 %all-gather.7.cloned.1.call-done = bf16[32,14,4096]{2,0,1:T(8,128)(2,1)} async-done(((bf16[8,14,4096]{2,0,1:T(8,128)(2,1)}), bf16[32,14,4096]{2,0,1:T(8,128)(2,1)}) %all-gather.7.cloned.1.call-update) | async-done | bytes 3670032 | tf_op jit(solution)/shard_map/all_gather | solution.py:51
  94.1 6.0 %copy.13 = bf16[32,14,4096]{2,1,0:T(8,128)(2,1)} copy(bf16[32,14,4096]{2,0,1:T(8,128)(2,1)} %all-gather.7.cloned.1.call-done) | data formatting | bytes 7340032 | tf_op jit(solution)/shard_map/all_gather | solution.py:51
  100.1 5.0 %reshape.122 = bf16[448,4096]{1,0:T(8,128)(2,1)} reshape(bf16[32,14,4096]{2,1,0:T(8,128)(2,1)} %copy.13) | data formatting | bytes 7340032 | tf_op jit(solution)/shard_map/reshape | solution.py:55
  105.1 5.5 %fusion.11 = (f32[448]{0:T(512)S(1)}, f32[448,501]{1,0:T(8,128)S(1)}) fusion(bf16[448,4096]{1,0:T(8,128)(2,1)} %reshape.122, bf16[4096,501]{0,1:T(8,128)(2,1)} %param.9), kind=kOutput, calls=%fused_computation.34 | convolution fusion | flops 1838902016 | bytes 8673792 | tf_op jit(solution)/shard_map/dot_general | solution.py:56
  110.5 3.1 %gather_fusion = f32[448]{0:T(512)S(1)} fusion(f32[448]{0:T(512)S(1)} %get-tuple-element.74, s32[1024]{0:T(1024)S(1)} %pad_clamp_fusion), kind=kCustom, calls=%fused_computation | custom fusion | bytes 5376 | tf_op jit(solution)/shard_map/gather | solution.py:67
  113.7 0.7 all_to_all.22
  114.4 3.2 %all-to-all-start = ((f32[4,1,112]{2,1,0:T(1,128)}), f32[4,1,112]{2,1,0:T(1,128)S(1)}, u32[]{:S(2)}, u32[]{:S(2)}) async-start(f32[4,1,112]{2,1,0:T(1,128)} %all_to_all.22), calls=%async_computation | async-start | bytes 4096 | tf_op jit(solution)/shard_map/all_to_all | solution.py:71
  117.6 0.5 select_reduce_fusion
  118.1 0.0 copy-start
  118.1 3.1 %gather_fusion.1 = f32[448]{0:T(512)S(1)} fusion(f32[448]{0:T(512)S(1)} %get-tuple-element.46, s32[1024]{0:T(1024)S(1)} %pad_clamp_fusion), kind=kCustom, calls=%fused_computation.1 | custom fusion | bytes 5376 | tf_op jit(solution)/shard_map/gather | solution.py:68
  121.2 0.7 all_to_all.24
  121.9 1.1 all-to-all-done
  123.1 3.9 %all-to-all-start.1 = ((f32[4,1,112]{2,1,0:T(1,128)}), f32[4,1,112]{2,1,0:T(1,128)S(1)}, u32[]{:S(2)}, u32[]{:S(2)}) async-start(f32[4,1,112]{2,1,0:T(1,128)} %all_to_all.24), calls=%async_computation.1 | async-start | bytes 4096 | tf_op jit(solution)/shard_map/all_to_all | solution.py:72
  127.0 0.1 dynamic-slice.3
  127.0 0.7 dynamic-slice_reduce_fusion
  127.7 0.0 copy-done
  127.7 0.6 dynamic-slice
  128.9 3.1 %gather_fusion.2 = f32[448]{0:T(512)S(1)} fusion(f32[448]{0:T(512)S(1)} %get-tuple-element.45, s32[1024]{0:T(1024)S(1)} %pad_clamp_fusion), kind=kCustom, calls=%fused_computation.2 | custom fusion | bytes 5376 | tf_op jit(solution)/shard_map/gather | solution.py:69
  132.1 0.7 all_to_all.28
  132.8 0.0 all-to-all-done.1
  132.8 5.1 %all-to-all-start.2 = ((f32[4,1,112]{2,1,0:T(1,128)}), f32[4,1,112]{2,1,0:T(1,128)S(1)}, u32[]{:S(2)}, u32[]{:S(2)}) async-start(f32[4,1,112]{2,1,0:T(1,128)} %all_to_all.28), calls=%async_computation.2 | async-start | bytes 4096 | tf_op jit(solution)/shard_map/all_to_all | solution.py:73
  137.9 0.2 dynamic-update-slice
  138.2 0.2 dynamic-update-slice.1
  138.4 5.0 %all-to-all-done.2 = f32[4,1,112]{2,1,0:T(1,128)S(1)} async-done(((f32[4,1,112]{2,1,0:T(1,128)}), f32[4,1,112]{2,1,0:T(1,128)S(1)}, u32[]{:S(2)}, u32[]{:S(2)}) %all-to-all-start.2) | async-done | bytes 1824 | tf_op jit(solution)/shard_map/all_to_all | solution.py:73
  143.4 0.2 dynamic-update-slice.2
  143.7 22.3 %all-reduce.3 = (f32[896]{0:T(1024)S(1)}, f32[896]{0:T(1024)S(1)}, f32[896]{0:T(1024)S(1)}) all-reduce(f32[896]{0:T(1024)S(1)} %dynamic-update-slice, f32[896]{0:T(1024)S(1)} %dynamic-update-slice.1, f32[896]{0:T(1024)S(1)} %dynamic-update-slice.2), channel_id=2, replica_groups=mesh['dp'=4,'vocab'=8] {'vocab'}, use_global_device_ids=true, to_apply=%add | all-reduce | flops 2688 | bytes 21504
  166.0 0.1 slice.27
  166.0 0.1 slice.28
  166.1 0.1 slice.29
  166.2 0.1 reshape.163
  166.3 0.1 reshape.164
  166.3 0.1 reshape.165
  166.4 0.3 while.14
  166.7 0.1 sub.60
  166.8 0.8 fusion.9
  167.6 1.2 convert_divide_fusion
  (21 shorter events, 0.3 us)
Async XLA Ops:
  7.2 87.0 %all-gather.7.cloned.1.call-start = ((), (), s32[]{:S(2)}) async-start(), calls=%async_computation.3 | async-start | bytes 4587520 | tf_op jit(solution)/shard_map/all_gather | solution.py:51
  114.4 8.7 %all-to-all-start = ((f32[4,1,112]{2,1,0:T(1,128)}), f32[4,1,112]{2,1,0:T(1,128)S(1)}, u32[]{:S(2)}, u32[]{:S(2)}) async-start(f32[4,1,112]{2,1,0:T(1,128)} %all_to_all.22), calls=%async_computation | async-start | bytes 4096 | tf_op jit(solution)/shard_map/all_to_all | solution.py:71
  118.1 9.6 %copy-start = (u32[32]{0:T(128)S(1)}, u32[32]{0:T(128)}, u32[]{:S(2)}) copy-start(u32[32]{0:T(128)} %constant.44) | copy-start | bytes 388
  123.1 9.7 %all-to-all-start.1 = ((f32[4,1,112]{2,1,0:T(1,128)}), f32[4,1,112]{2,1,0:T(1,128)S(1)}, u32[]{:S(2)}, u32[]{:S(2)}) async-start(f32[4,1,112]{2,1,0:T(1,128)} %all_to_all.24), calls=%async_computation.1 | async-start | bytes 4096 | tf_op jit(solution)/shard_map/all_to_all | solution.py:72
  132.8 10.6 %all-to-all-start.2 = ((f32[4,1,112]{2,1,0:T(1,128)}), f32[4,1,112]{2,1,0:T(1,128)S(1)}, u32[]{:S(2)}, u32[]{:S(2)}) async-start(f32[4,1,112]{2,1,0:T(1,128)} %all_to_all.28), calls=%async_computation.2 | async-start | bytes 4096 | tf_op jit(solution)/shard_map/all_to_all | solution.py:73
Sparse Core Ops, SparseCore 0:
  21.5 72.5 all-gather.6
where the time goes:
time: 176 us
  blocking collectives  70.1 us (40%)
  waiting for transfers between devices  42.2 us (24%)
  local copies, waits for them, and re-layouts  25.2 us (14%)
  between operations  14.8 us (8%)
  starting transfers between devices  12.3 us (7%)
  other arithmetic  5.56 us (3%)
  matrix products  5.47 us (3%)
    all_gather x1, waiting for transfers between devices, local(): lax.all_gather(features, 'dp', axis=0, tiled=True)  36 us
    unnamed x1, blocking collectives  22.3 us
    all_gather x1, blocking collectives, local(): features = lax.all_gather(hidden, 'vocab', axis=2, tiled=True)  14.2 us
    all_gather x1, blocking collectives, local(): lax.all_gather(targets, 'dp', axis=0, tiled=True)  14.1 us
    all_gather x1, blocking collectives, local(): lax.all_gather(rewards, 'dp', axis=0, tiled=True)  11.3 us
    all_gather x1, blocking collectives, local(): lax.all_gather(lengths, 'dp', axis=0, tiled=True)  8.2 us
    all_gather x1, local copies, waits for them, and re-layouts, local(): lax.all_gather(features, 'dp', axis=0, tiled=True)  5.99 us
    dot_general x1, matrix products, local(): logits = jnp.dot(row_block, weight, preferred_element_type=jnp.float32)  5.47 us
  transfers between devices with their start and end apart: 4, of which 3 were waited for; matrix products, arithmetic and copies ran while one was open for 7% of the time, Pallas kernels for 0%

commit v1 on v0

--- a/solution.py
+++ b/solution.py
@@ -2,6 +2,7 @@
 import jax.numpy as jnp
 from jax import lax
 from jax.sharding import PartitionSpec as P
+from jax.lax import axis_index, axis_size, ppermute
 
 SAMPLES = 8
 reward_unit = 1.0 / 64.0
@@ -34,7 +35,16 @@
         lax.all_gather(lengths, "dp", axis=0, tiled=True),
         lax.all_gather(rewards, "dp", axis=0, tiled=True),
     )
-    features = lax.all_gather(hidden, "vocab", axis=2, tiled=True)
+    ndev = axis_size("vocab")
+    main = sorted(((jj, (jj + 1) % ndev) for jj in range(ndev)))
+    prior = hidden
+    row_list = [prior]
+    for num in range(1, ndev):
+        prior = ppermute(prior, "vocab", perm=main)
+        row_list.insert(0, prior)
+    carry_out = jnp.concatenate(row_list, 2)
+    f_next = axis_index("vocab") + 1
+    features = jnp.roll(carry_out, f_next * hidden.shape[2], 2)
     model_width = features.shape[2]
     column_ids = lax.iota(jnp.int32, shard_width)
     position_ids = lax.iota(jnp.int32, window)

time: 176 us -> 200 us (1.14)
  waiting for transfers between devices: 42.2 us -> 79.8 us
  blocking collectives: 70.1 us -> 56 us
  local copies, waits for them, and re-layouts: 25.2 us -> 27.3 us
    ppermute x0 -> x7, waiting for transfers between devices: none -> 36.2 us  [local(): prior = ppermute(prior, 'vocab', perm=main)]
    all_gather x1 -> x0, blocking collectives: 14.2 us -> none  [local(): features = lax.all_gather(hidden, 'vocab', axis=2, tiled=True)]
    all_gather x1, blocking collectives: 8.2 us -> 11.9 us  [local(): lax.all_gather(lengths, 'dp', axis=0, tiled=True)]
    all_to_all x1, waiting for transfers between devices: 5.01 us -> 1.56 us  [local(): lax.all_to_all(ordered_picked, 'dp', split_axis=0, concat_axis=0, tiled=T...]
    all_gather x1, blocking collectives: 11.3 us -> 7.99 us  [local(): lax.all_gather(rewards, 'dp', axis=0, tiled=True)]
    all_to_all x1, waiting for transfers between devices: 0.01 us -> 2.89 us  [local(): lax.all_to_all(ordered_totals, 'dp', split_axis=0, concat_axis=0, tiled=T...]
  transfers between devices with their start and end apart: 4 -> 11, of which waited for: 3 -> 11; matrix products, arithmetic and copies ran while one was open for 7% -> 5% of each run, Pallas kernels for 0% -> 0%
where the time goes in v1:
time: 200 us; the launch traced here: 199 us
  waiting for transfers between devices  79.8 us (40%)
  blocking collectives  56 us (28%)
  local copies, waits for them, and re-layouts  27.3 us (14%)
  between operations  15 us (8%)
  starting transfers between devices  10.8 us (5%)
  matrix products  5.47 us (3%)
  other arithmetic  4.92 us (2%)
    all_gather x1, waiting for transfers between devices, local(): lax.all_gather(features, 'dp', axis=0, tiled=True)  37.4 us
    ppermute x7, waiting for transfers between devices, local(): prior = ppermute(prior, 'vocab', perm=main)  36.2 us
    unnamed x1, blocking collectives  22.3 us
    all_gather x1, blocking collectives, local(): lax.all_gather(targets, 'dp', axis=0, tiled=True)  13.8 us
    all_gather x1, blocking collectives, local(): lax.all_gather(lengths, 'dp', axis=0, tiled=True)  11.9 us
    all_gather x1, blocking collectives, local(): lax.all_gather(rewards, 'dp', axis=0, tiled=True)  7.99 us
    all_gather x1, local copies, waits for them, and re-layouts, local(): lax.all_gather(features, 'dp', axis=0, tiled=True)  5.99 us
    dot_general x1, matrix products, local(): logits = jnp.dot(row_block, weight, preferred_element_type=jnp.float32)  5.47 us
  transfers between devices with their start and end apart: 11, of which 11 were waited for; matrix products, arithmetic and copies ran while one was open for 5% of the time, Pallas kernels for 0%

profile of v1, /device:TPU:0, one launch (start us, length us, event | category | flops | bytes accessed | tf_op | source)
XLA Modules:
  0.0 199.3 jit_solution(11706684218137407399)
XLA Ops:
  7.2 0.0 copy-start
  7.2 0.0 all-gather.7.cloned.1.call-start
  7.2 0.5 collective-permute-start
  7.8 5.6 %collective-permute-done = bf16[8,14,512]{2,0,1:T(8,128)(2,1)S(1)} collective-permute-done((bf16[8,14,512]{2,0,1:T(8,128)(2,1)}, bf16[8,14,512]{2,0,1:T(8,128)(2,1)S(1)}, u32[]{:S(2)}, u32[]{:S(2)}) %collective-permute-start) | collective-permute-done | bytes 114720 | tf_op jit(solution)/shard_map/ppermute | solution.py:43
  13.3 0.0 collective-permute-start.1
  13.3 5.1 %collective-permute-done.1 = bf16[8,14,512]{2,0,1:T(8,128)(2,1)S(1)} collective-permute-done((bf16[8,14,512]{2,0,1:T(8,128)(2,1)S(1)}, bf16[8,14,512]{2,0,1:T(8,128)(2,1)S(1)}, u32[]{:S(2)}, u32[]{:S(2)}) %collective-permute-start.1) | collective-permute-done | bytes 114720 | tf_op jit(solution)/shard_map/ppermute | solution.py:43
  18.4 5.1 %collective-permute-done.2 = bf16[8,14,512]{2,0,1:T(8,128)(2,1)S(1)} collective-permute-done((bf16[8,14,512]{2,0,1:T(8,128)(2,1)S(1)}, bf16[8,14,512]{2,0,1:T(8,128)(2,1)S(1)}, u32[]{:S(2)}, u32[]{:S(2)}) %collective-permute-start.2) | collective-permute-done | bytes 114720 | tf_op jit(solution)/shard_map/ppermute | solution.py:43
  23.6 5.1 %collective-permute-done.3 = bf16[8,14,512]{2,0,1:T(8,128)(2,1)S(1)} collective-permute-done((bf16[8,14,512]{2,0,1:T(8,128)(2,1)S(1)}, bf16[8,14,512]{2,0,1:T(8,128)(2,1)S(1)}, u32[]{:S(2)}, u32[]{:S(2)}) %collective-permute-start.3) | collective-permute-done | bytes 114720 | tf_op jit(solution)/shard_map/ppermute | solution.py:43
  28.7 5.1 %collective-permute-done.4 = bf16[8,14,512]{2,0,1:T(8,128)(2,1)S(1)} collective-permute-done((bf16[8,14,512]{2,0,1:T(8,128)(2,1)S(1)}, bf16[8,14,512]{2,0,1:T(8,128)(2,1)S(1)}, u32[]{:S(2)}, u32[]{:S(2)}) %collective-permute-start.4) | collective-permute-done | bytes 114720 | tf_op jit(solution)/shard_map/ppermute | solution.py:43
  33.8 5.1 %collective-permute-done.5 = bf16[8,14,512]{2,0,1:T(8,128)(2,1)S(1)} collective-permute-done((bf16[8,14,512]{2,0,1:T(8,128)(2,1)S(1)}, bf16[8,14,512]{2,0,1:T(8,128)(2,1)S(1)}, u32[]{:S(2)}, u32[]{:S(2)}) %collective-permute-start.5) | collective-permute-done | bytes 114720 | tf_op jit(solution)/shard_map/ppermute | solution.py:43
  38.9 5.1 %collective-permute-done.6 = bf16[8,14,512]{2,0,1:T(8,128)(2,1)S(1)} collective-permute-done((bf16[8,14,512]{2,0,1:T(8,128)(2,1)S(1)}, bf16[8,14,512]{2,0,1:T(8,128)(2,1)S(1)}, u32[]{:S(2)}, u32[]{:S(2)}) %collective-permute-start.6) | collective-permute-done | bytes 114720 | tf_op jit(solution)/shard_map/ppermute | solution.py:43
  44.1 0.9 constant_dynamic-update-slice_fusion.8
  45.1 0.0 copy-start.2
  45.1 0.0 copy-start.3
  45.1 0.0 copy-start.1
  45.2 0.0 copy-start.4
  45.3 1.0 constant_dynamic-slice_fusion.3
  46.3 0.0 all-gather.7.cloned.1.call-update
  46.3 11.9 %all-gather.3 = s32[4,1,8]{2,1,0:T(1,128)S(1)} all-gather(s32[1,1,8]{2,1,0:T(1,128)S(1)} %bitcast.32), channel_id=1, replica_groups=mesh['dp'=4,'vocab'=8] {'dp'}, dimensions={0}, use_global_device_ids=true | all-gather | bytes 160 | tf_op jit(solution)/shard_map/all_gather | solution.py:35
  58.2 8.0 %all-gather.4 = s32[4,1,8]{2,1,0:T(1,128)S(1)} all-gather(s32[1,1,8]{2,1,0:T(1,128)S(1)} %bitcast.33), channel_id=1, replica_groups=mesh['dp'=4,'vocab'=8] {'dp'}, dimensions={0}, use_global_device_ids=true | all-gather | bytes 160 | tf_op jit(solution)/shard_map/all_gather | solution.py:36
  66.2 13.8 %all_gather.36 = s32[32,14]{1,0:T(8,128)S(1)} all-gather(s32[8,14]{1,0:T(8,128)S(1)} %copy-done.1), channel_id=1, replica_groups=mesh['dp'=4,'vocab'=8] {'dp'}, dimensions={0}, use_global_device_ids=true | all-gather | bytes 2240 | tf_op jit(solution)/shard_map/all_gather | solution.py:62
  80.0 0.1 sub.62
  80.1 0.5 broadcast.117
  80.6 0.7 reduce.10
  81.3 0.1 broadcast_in_dim.55
  81.3 0.7 reduce.11
  82.0 0.1 broadcast_in_dim.62
  82.1 0.1 select_reduce_fusion.1
  82.2 0.1 compare_select_fusion
  82.3 0.1 reshape.126
  82.5 37.4 %all-gather.7.cloned.1.call-done = bf16[32,14,4096]{2,0,1:T(8,128)(2,1)} async-done(((bf16[8,14,4096]{2,0,1:T(8,128)(2,1)}), bf16[32,14,4096]{2,0,1:T(8,128)(2,1)}) %all-gather.7.cloned.1.call-update) | async-done | bytes 3670032 | tf_op jit(solution)/shard_map/all_gather | solution.py:61
  119.8 6.0 %copy.13 = bf16[32,14,4096]{2,1,0:T(8,128)(2,1)} copy(bf16[32,14,4096]{2,0,1:T(8,128)(2,1)} %all-gather.7.cloned.1.call-done) | data formatting | bytes 7340032 | tf_op jit(solution)/shard_map/all_gather | solution.py:61
  125.8 5.0 %reshape.122 = bf16[448,4096]{1,0:T(8,128)(2,1)} reshape(bf16[32,14,4096]{2,1,0:T(8,128)(2,1)} %copy.13) | data formatting | bytes 7340032 | tf_op jit(solution)/shard_map/reshape | solution.py:65
  130.8 5.5 %fusion.11 = (f32[448]{0:T(512)S(1)}, f32[448,501]{1,0:T(8,128)S(1)}) fusion(bf16[448,4096]{1,0:T(8,128)(2,1)} %reshape.122, bf16[4096,501]{0,1:T(8,128)(2,1)} %param.9), kind=kOutput, calls=%fused_computation.51 | convolution fusion | flops 1838902016 | bytes 8673792 | tf_op jit(solution)/shard_map/dot_general | solution.py:66
  136.3 0.5 select_reduce_fusion
  136.7 3.2 %gather_fusion.2 = f32[448]{0:T(512)S(1)} fusion(f32[448]{0:T(512)S(1)} %get-tuple-element.45, s32[1024]{0:T(1024)S(1)} %pad_clamp_fusion), kind=kCustom, calls=%fused_computation.2 | custom fusion | bytes 5376 | tf_op jit(solution)/shard_map/gather | solution.py:79
  139.9 0.7 all_to_all.28
  140.6 3.2 %all-to-all-start.2 = ((f32[4,1,112]{2,1,0:T(1,128)}), f32[4,1,112]{2,1,0:T(1,128)S(1)}, u32[]{:S(2)}, u32[]{:S(2)}) async-start(f32[4,1,112]{2,1,0:T(1,128)} %all_to_all.28), calls=%async_computation.2 | async-start | bytes 4096 | tf_op jit(solution)/shard_map/all_to_all | solution.py:83
  143.8 3.2 %gather_fusion = f32[448]{0:T(512)S(1)} fusion(f32[448]{0:T(512)S(1)} %get-tuple-element.74, s32[1024]{0:T(1024)S(1)} %pad_clamp_fusion), kind=kCustom, calls=%fused_computation | custom fusion | bytes 5376 | tf_op jit(solution)/shard_map/gather | solution.py:77
  147.0 0.7 all_to_all.22
  147.7 1.6 all-to-all-done.2
  149.2 3.5 %all-to-all-start = ((f32[4,1,112]{2,1,0:T(1,128)}), f32[4,1,112]{2,1,0:T(1,128)S(1)}, u32[]{:S(2)}, u32[]{:S(2)}) async-start(f32[4,1,112]{2,1,0:T(1,128)} %all_to_all.22), calls=%async_computation | async-start | bytes 4096 | tf_op jit(solution)/shard_map/all_to_all | solution.py:81
  152.7 3.2 %gather_fusion.1 = f32[448]{0:T(512)S(1)} fusion(f32[448]{0:T(512)S(1)} %get-tuple-element.46, s32[1024]{0:T(1024)S(1)} %pad_clamp_fusion), kind=kCustom, calls=%fused_computation.1 | custom fusion | bytes 5376 | tf_op jit(solution)/shard_map/gather | solution.py:78
  155.9 0.7 all_to_all.24
  156.6 1.7 all-to-all-done
  158.2 3.4 %all-to-all-start.1 = ((f32[4,1,112]{2,1,0:T(1,128)}), f32[4,1,112]{2,1,0:T(1,128)S(1)}, u32[]{:S(2)}, u32[]{:S(2)}) async-start(f32[4,1,112]{2,1,0:T(1,128)} %all_to_all.24), calls=%async_computation.1 | async-start | bytes 4096 | tf_op jit(solution)/shard_map/all_to_all | solution.py:82
  161.7 0.1 dynamic-slice.3
  161.7 0.7 dynamic-slice_reduce_fusion
  162.4 0.6 dynamic-slice
  163.7 0.2 dynamic-update-slice.2
  163.9 0.2 dynamic-update-slice
  164.2 2.9 %all-to-all-done.1 = f32[4,1,112]{2,1,0:T(1,128)S(1)} async-done(((f32[4,1,112]{2,1,0:T(1,128)}), f32[4,1,112]{2,1,0:T(1,128)S(1)}, u32[]{:S(2)}, u32[]{:S(2)}) %all-to-all-start.1) | async-done | bytes 1824 | tf_op jit(solution)/shard_map/all_to_all | solution.py:82
  167.1 0.2 dynamic-update-slice.1
  167.4 22.3 %all-reduce.3 = (f32[896]{0:T(1024)S(1)}, f32[896]{0:T(1024)S(1)}, f32[896]{0:T(1024)S(1)}) all-reduce(f32[896]{0:T(1024)S(1)} %dynamic-update-slice, f32[896]{0:T(1024)S(1)} %dynamic-update-slice.1, f32[896]{0:T(1024)S(1)} %dynamic-update-slice.2), channel_id=2, replica_groups=mesh['dp'=4,'vocab'=8] {'vocab'}, use_global_device_ids=true, to_apply=%add | all-reduce | flops 2688 | bytes 21504
  189.7 0.1 slice.27
  189.7 0.1 slice.28
  189.8 0.1 slice.29
  189.9 0.1 reshape.163
  190.0 0.1 reshape.164
  190.0 0.1 reshape.165
  190.1 0.3 while.14
  190.4 0.1 sub.65
  190.5 0.8 fusion.9
  191.3 1.2 convert_divide_fusion
  (48 shorter events, 0.5 us)
Async XLA Ops:
  7.2 38.1 %copy-start = (bf16[8,14,512]{2,0,1:T(8,128)(2,1)S(1)}, bf16[8,14,512]{2,0,1:T(8,128)(2,1)}, u32[]{:S(2)}) copy-start(bf16[8,14,512]{2,0,1:T(8,128)(2,1)} %param.8) | copy-start | bytes 344068
  7.2 112.7 %all-gather.7.cloned.1.call-start = ((), (), s32[]{:S(2)}) async-start(), calls=%async_computation.3 | async-start | bytes 4587520 | tf_op jit(solution)/shard_map/all_gather | solution.py:61
  7.2 6.1 %collective-permute-start = (bf16[8,14,512]{2,0,1:T(8,128)(2,1)}, bf16[8,14,512]{2,0,1:T(8,128)(2,1)S(1)}, u32[]{:S(2)}, u32[]{:S(2)}) collective-permute-start(bf16[8,14,512]{2,0,1:T(8,128)(2,1)} %param.8), channel_id=1, source_target_pairs={{0,1},{1,2},{2,3},{3,4},{4,5},{5,6},{6,7},{7,0},{8,9},{9,10},{10,1... | collective-permute-start | bytes 344072 | tf_op jit(solution)/shard_map/ppermute | solution.py:43
  13.3 5.1 %collective-permute-start.1 = (bf16[8,14,512]{2,0,1:T(8,128)(2,1)S(1)}, bf16[8,14,512]{2,0,1:T(8,128)(2,1)S(1)}, u32[]{:S(2)}, u32[]{:S(2)}) collective-permute-start(bf16[8,14,512]{2,0,1:T(8,128)(2,1)S(1)} %collective-permute-done), channel_id=1, source_target_pairs={{0,1},{1,2},{2,3},{3,4},{4,5},{5,6},{6,7},{7,0},{8,9},{9,10},{10,1... | collective-permute-start | bytes 344072 | tf_op jit(solution)/shard_map/ppermute | solution.py:43
  18.4 5.1 %collective-permute-start.2 = (bf16[8,14,512]{2,0,1:T(8,128)(2,1)S(1)}, bf16[8,14,512]{2,0,1:T(8,128)(2,1)S(1)}, u32[]{:S(2)}, u32[]{:S(2)}) collective-permute-start(bf16[8,14,512]{2,0,1:T(8,128)(2,1)S(1)} %collective-permute-done.1), channel_id=1, source_target_pairs={{0,1},{1,2},{2,3},{3,4},{4,5},{5,6},{6,7},{7,0},{8,9},{9,10},{10,1... | collective-permute-start | bytes 344072 | tf_op jit(solution)/shard_map/ppermute | solution.py:43
  23.6 5.1 %collective-permute-start.3 = (bf16[8,14,512]{2,0,1:T(8,128)(2,1)S(1)}, bf16[8,14,512]{2,0,1:T(8,128)(2,1)S(1)}, u32[]{:S(2)}, u32[]{:S(2)}) collective-permute-start(bf16[8,14,512]{2,0,1:T(8,128)(2,1)S(1)} %collective-permute-done.2), channel_id=1, source_target_pairs={{0,1},{1,2},{2,3},{3,4},{4,5},{5,6},{6,7},{7,0},{8,9},{9,10},{10,1... | collective-permute-start | bytes 344072 | tf_op jit(solution)/shard_map/ppermute | solution.py:43
  28.7 5.1 %collective-permute-start.4 = (bf16[8,14,512]{2,0,1:T(8,128)(2,1)S(1)}, bf16[8,14,512]{2,0,1:T(8,128)(2,1)S(1)}, u32[]{:S(2)}, u32[]{:S(2)}) collective-permute-start(bf16[8,14,512]{2,0,1:T(8,128)(2,1)S(1)} %collective-permute-done.3), channel_id=1, source_target_pairs={{0,1},{1,2},{2,3},{3,4},{4,5},{5,6},{6,7},{7,0},{8,9},{9,10},{10,1... | collective-permute-start | bytes 344072 | tf_op jit(solution)/shard_map/ppermute | solution.py:43
  33.8 5.1 %collective-permute-start.5 = (bf16[8,14,512]{2,0,1:T(8,128)(2,1)S(1)}, bf16[8,14,512]{2,0,1:T(8,128)(2,1)S(1)}, u32[]{:S(2)}, u32[]{:S(2)}) collective-permute-start(bf16[8,14,512]{2,0,1:T(8,128)(2,1)S(1)} %collective-permute-done.4), channel_id=1, source_target_pairs={{0,1},{1,2},{2,3},{3,4},{4,5},{5,6},{6,7},{7,0},{8,9},{9,10},{10,1... | collective-permute-start | bytes 344072 | tf_op jit(solution)/shard_map/ppermute | solution.py:43
  38.9 5.1 %collective-permute-start.6 = (bf16[8,14,512]{2,0,1:T(8,128)(2,1)S(1)}, bf16[8,14,512]{2,0,1:T(8,128)(2,1)S(1)}, u32[]{:S(2)}, u32[]{:S(2)}) collective-permute-start(bf16[8,14,512]{2,0,1:T(8,128)(2,1)S(1)} %collective-permute-done.5), channel_id=1, source_target_pairs={{0,1},{1,2},{2,3},{3,4},{4,5},{5,6},{6,7},{7,0},{8,9},{9,10},{10,1... | collective-permute-start | bytes 344072 | tf_op jit(solution)/shard_map/ppermute | solution.py:43
  45.1 1.2 copy-start.2
  45.1 13.1 %copy-start.3 = (s32[1,8]{1,0:T(1,128)S(1)}, s32[1,8]{1,0:T(1,128)}, u32[]{:S(2)}) copy-start(s32[1,8]{1,0:T(1,128)} %param.12) | copy-start | bytes 100
  45.1 21.0 %copy-start.1 = (s32[8,14]{1,0:T(8,128)S(1)}, s32[8,14]{1,0:T(8,128)}, u32[]{:S(2)}) copy-start(s32[8,14]{1,0:T(8,128)} %param.10) | copy-start | bytes 1348
  45.2 36.9 %copy-start.4 = (s32[32]{0:T(128)S(1)}, s32[32]{0:T(128)}, u32[]{:S(2)}) copy-start(s32[32]{0:T(128)} %param.13) | copy-start | bytes 388
  140.6 8.6 %all-to-all-start.2 = ((f32[4,1,112]{2,1,0:T(1,128)}), f32[4,1,112]{2,1,0:T(1,128)S(1)}, u32[]{:S(2)}, u32[]{:S(2)}) async-start(f32[4,1,112]{2,1,0:T(1,128)} %all_to_all.28), calls=%async_computation.2 | async-start | bytes 4096 | tf_op jit(solution)/shard_map/all_to_all | solution.py:83
  149.2 9.0 %all-to-all-start = ((f32[4,1,112]{2,1,0:T(1,128)}), f32[4,1,112]{2,1,0:T(1,128)S(1)}, u32[]{:S(2)}, u32[]{:S(2)}) async-start(f32[4,1,112]{2,1,0:T(1,128)} %all_to_all.22), calls=%async_computation | async-start | bytes 4096 | tf_op jit(solution)/shard_map/all_to_all | solution.py:81
  152.7 9.7 %copy-start.5 = (u32[32]{0:T(128)S(1)}, u32[32]{0:T(128)}, u32[]{:S(2)}) copy-start(u32[32]{0:T(128)} %constant.69) | copy-start | bytes 388
  158.2 8.9 %all-to-all-start.1 = ((f32[4,1,112]{2,1,0:T(1,128)}), f32[4,1,112]{2,1,0:T(1,128)S(1)}, u32[]{:S(2)}, u32[]{:S(2)}) async-start(f32[4,1,112]{2,1,0:T(1,128)} %all_to_all.24), calls=%async_computation.1 | async-start | bytes 4096 | tf_op jit(solution)/shard_map/all_to_all | solution.py:82
Sparse Core Ops, SparseCore 0:
  46.4 73.4 all-gather.6
